TPU v7x, 32 devices: a whole 2x2x4 slice. The times are simulated.
32 devices in a mesh: job: 2 (over core), replica: 4 (over z), model: 4 (over y, x).
Axes of the slice: x: 2, y: 2, z: 4, core: 2. Of those that a mesh axis runs over, the one named last changes fastest.
Arguments:
- grad_query: float32 [8, 1024, 1024], P(('job', 'replica'), None, 'model'), parts along dimension 0, may hold values from -0.875 to 0.875
- grad_key: float32 [8, 1024, 1024], P(('job', 'replica'), None, 'model'), parts along dimension 0, may hold values from -0.875 to 0.875
- grad_value: float32 [8, 1024, 1024], P(('job', 'replica'), None, 'model'), parts along dimension 0, may hold values from -0.875 to 0.875
- grad_mixed: float32 [8, 1024, 1024], P(('job', 'replica'), 'model'), parts along dimension 0, may hold values from -0.875 to 0.875
- grad_norm: float32 [8, 1024], P(('job', 'replica')), parts along dimension 0, may hold values from -8 to 8
- weight_query: float32 [2048, 1024], P(('job', 'replica'), 'model'), parts along dimension 0, may hold values from -0.25 to 0.25
- weight_key: float32 [2048, 1024], P(('job', 'replica'), 'model'), parts along dimension 0, may hold values from -0.25 to 0.25
- weight_value: float32 [2048, 1024], P(('job', 'replica'), 'model'), parts along dimension 0, may hold values from -0.25 to 0.25
- weight_mixed: float32 [2048, 1024], P(('job', 'model'), 'replica'), parts along dimension 0, may hold values from -0.25 to 0.25
- weight_norm: float32 [2048], P(('job', 'replica')), parts along dimension 0, may hold values from 0.25 to 1.75
- moment_query: float32 [2048, 1024], P(('job', 'replica'), 'model'), parts along dimension 0, may hold values from -0.1875 to 0.1875
- moment_key: float32 [2048, 1024], P(('job', 'replica'), 'model'), parts along dimension 0, may hold values from -0.1875 to 0.1875
- moment_value: float32 [2048, 1024], P(('job', 'replica'), 'model'), parts along dimension 0, may hold values from -0.1875 to 0.1875
- moment_mixed: float32 [2048, 1024], P(('job', 'model'), 'replica'), parts along dimension 0, may hold values from -0.1875 to 0.1875
- moment_norm: float32 [2048], P(('job', 'replica')), parts along dimension 0, may hold values from -1.75 to 1.75
Outputs:
- copy_query: bfloat16 [2048, 1024], P('job', 'model'), parts along dimension 0
- copy_key: bfloat16 [2048, 1024], P('job', 'model'), parts along dimension 0
- copy_value: bfloat16 [2048, 1024], P('job', 'model'), parts along dimension 0
- copy_mixed: bfloat16 [2048, 1024], P(('job', 'model')), parts along dimension 0
- copy_norm: bfloat16 [2048], P('job'), parts along dimension 0
- new_query: float32 [2048, 1024], P(('job', 'replica'), 'model'), parts along dimension 0
- new_key: float32 [2048, 1024], P(('job', 'replica'), 'model'), parts along dimension 0
- new_value: float32 [2048, 1024], P(('job', 'replica'), 'model'), parts along dimension 0
- new_mixed: float32 [2048, 1024], P(('job', 'model'), 'replica'), parts along dimension 0
- new_norm: float32 [2048], P(('job', 'replica')), parts along dimension 0
- state_new_query: float32 [2048, 1024], P(('job', 'replica'), 'model'), parts along dimension 0
- state_new_key: float32 [2048, 1024], P(('job', 'replica'), 'model'), parts along dimension 0
- state_new_value: float32 [2048, 1024], P(('job', 'replica'), 'model'), parts along dimension 0
- state_new_mixed: float32 [2048, 1024], P(('job', 'model'), 'replica'), parts along dimension 0
- state_new_norm: float32 [2048], P(('job', 'replica')), parts along dimension 0
There are 2 independent parts, one for each index of `job`. A program takes and returns all parts, laid end to end along the dimension named above; each array names one. Nothing has to cross between parts.
All inputs are finite; a program needn't handle non-finite values.
Results may differ from a plain program's by a relative error of at most 0.0004.
Values may be sent and summed in bfloat16 or wider, within the bound.
No kernel may reach another device: no remote copies, remote signals or barrier semaphores. Data moves between devices by JAX's collectives and lax.ppermute only.
A program may use at most 64 MiB of HBM per device.

v0:
```python
import jax
import jax.numpy as jnp
from jax import lax
from jax.sharding import PartitionSpec as P

learn_rate = 0.5
hold_rate = 0.9


def local(
    grad_query,
    grad_key,
    grad_value,
    grad_mixed,
    grad_norm,
    weight_query,
    weight_key,
    weight_value,
    weight_mixed,
    weight_norm,
    moment_query,
    moment_key,
    moment_value,
    moment_mixed,
    moment_norm,
):
    mean_query, mean_key, mean_value, mean_mixed = (
        lax.psum_scatter(grad_query[0], "replica", scatter_dimension=0, tiled=True),
        lax.psum_scatter(grad_key[0], "replica", scatter_dimension=0, tiled=True),
        lax.psum_scatter(grad_value[0], "replica", scatter_dimension=0, tiled=True),
        lax.psum_scatter(grad_mixed[0], "replica", scatter_dimension=1, tiled=True),
    )
    whole_norm = lax.psum(grad_norm[0], "replica")
    place = lax.axis_index("replica")
    mean_norm = lax.dynamic_slice_in_dim(
        whole_norm, place * weight_norm.shape[0], weight_norm.shape[0]
    )
    mean_rate = lax.axis_size("replica") ** (-0.5)
    mean_query = mean_query * mean_rate
    mean_key = mean_key * mean_rate
    mean_value = mean_value * mean_rate
    mean_mixed = mean_mixed * mean_rate
    mean_norm = mean_norm * mean_rate
    (
        own_query,
        own_key,
        own_value,
        own_mixed,
        slope_query_norm,
        slope_key_norm,
        slope_value_norm,
        slope_mixed_norm,
    ) = lax.psum(
        (
            jnp.sum(weight_query * weight_query, axis=1, keepdims=True),
            jnp.sum(weight_key * weight_key, axis=1, keepdims=True),
            jnp.sum(weight_value * weight_value, axis=1, keepdims=True),
            jnp.sum(weight_mixed * weight_mixed, axis=0, keepdims=True),
            jnp.sum(mean_query * mean_query, axis=1, keepdims=True),
            jnp.sum(mean_key * mean_key, axis=1, keepdims=True),
            jnp.sum(mean_value * mean_value, axis=1, keepdims=True),
            jnp.sum(mean_mixed * mean_mixed, axis=0, keepdims=True),
        ),
        "model",
    )
    mean_query = mean_query * (jnp.sqrt(own_query) * lax.rsqrt(slope_query_norm + 1e-06))
    mean_key = mean_key * (jnp.sqrt(own_key) * lax.rsqrt(slope_key_norm + 1e-06))
    mean_value = mean_value * (jnp.sqrt(own_value) * lax.rsqrt(slope_value_norm + 1e-06))
    mean_mixed = mean_mixed * (jnp.sqrt(own_mixed) * lax.rsqrt(slope_mixed_norm + 1e-06))
    state_new_query = hold_rate * moment_query + mean_query
    new_query = weight_query - learn_rate * state_new_query
    state_new_key = hold_rate * moment_key + mean_key
    new_key = weight_key - learn_rate * state_new_key
    state_new_value = hold_rate * moment_value + mean_value
    new_value = weight_value - learn_rate * state_new_value
    state_new_mixed = hold_rate * moment_mixed + mean_mixed
    new_mixed = weight_mixed - learn_rate * state_new_mixed
    state_new_norm = hold_rate * moment_norm + mean_norm
    new_norm = weight_norm - learn_rate * state_new_norm
    copy_query, copy_key, copy_value, copy_mixed, copy_norm = (
        lax.all_gather(new_query.astype(jnp.bfloat16), "replica", axis=0, tiled=True),
        lax.all_gather(new_key.astype(jnp.bfloat16), "replica", axis=0, tiled=True),
        lax.all_gather(new_value.astype(jnp.bfloat16), "replica", axis=0, tiled=True),
        lax.all_gather(new_mixed.astype(jnp.bfloat16), "replica", axis=1, tiled=True),
        lax.all_gather(new_norm.astype(jnp.bfloat16), "replica", axis=0, tiled=True),
    )
    return (
        copy_query,
        copy_key,
        copy_value,
        copy_mixed,
        copy_norm,
        new_query,
        new_key,
        new_value,
        new_mixed,
        new_norm,
        state_new_query,
        state_new_key,
        state_new_value,
        state_new_mixed,
        state_new_norm,
    )


def solution(mesh):
    placed = (
        P(("job", "replica"), None, "model"),
        P(("job", "replica"), None, "model"),
        P(("job", "replica"), None, "model"),
        P(("job", "replica"), "model", None),
        P(("job", "replica"), None),
        P(("job", "replica"), "model"),
        P(("job", "replica"), "model"),
        P(("job", "replica"), "model"),
        P(("job", "model"), "replica"),
        P(("job", "replica")),
        P(("job", "replica"), "model"),
        P(("job", "replica"), "model"),
        P(("job", "replica"), "model"),
        P(("job", "model"), "replica"),
        P(("job", "replica")),
    )
    return jax.shard_map(
        local,
        mesh=mesh,
        in_specs=placed,
        out_specs=(
            P("job", "model"),
            P("job", "model"),
            P("job", "model"),
            P(("job", "model"), None),
            P("job"),
            P(("job", "replica"), "model"),
            P(("job", "replica"), "model"),
            P(("job", "replica"), "model"),
            P(("job", "model"), "replica"),
            P(("job", "replica")),
            P(("job", "replica"), "model"),
            P(("job", "replica"), "model"),
            P(("job", "replica"), "model"),
            P(("job", "model"), "replica"),
            P(("job", "replica")),
        ),
        check_vma=False,
    )
```

profile of v0, /device:TPU:0, one launch (start us, length us, event | category | flops | bytes accessed | tf_op | source)
XLA Modules:
  0.0 210.1 jit_solution(8399502176376450542)
XLA Ops:
  7.2 0.7 reduce-scatter.9.cloned.1.call-update
  8.0 0.7 reduce-scatter.11.cloned.1.call-update
  8.7 0.7 reduce-scatter.5.cloned.1.call-update
  9.5 0.5 reduce-scatter.7.cloned.1.call-update
  10.0 0.1 copy-done.12
  10.1 13.5 %psum.71 = f32[1024]{0:T(1024)S(1)} all-reduce(f32[1024]{0:T(1024)S(1)} %bitcast.36), channel_id=1, replica_groups=mesh['job'=2,'replica'=4,'model'=4] {'replica'}, use_global_device_ids=true, to_apply=%region_20.0 | all-reduce | flops 1024 | bytes 8192 | tf_op jit(solution)/shard_map/psum | solution.py:33
  23.6 0.6 fusion
  24.3 7.7 %all-gather = bf16[4,1,256]{2,1,0:T(2,128)(2,1)S(1)} all-gather(bf16[1,1,256]{2,1,0:T(2,128)(2,1)S(1)} %reshape.38), channel_id=1, replica_groups=mesh['job'=2,'replica'=4,'model'=4] {'replica'}, dimensions={0}, use_global_device_ids=true | all-gather | bytes 2560 | tf_op jit(solution)/shard_map/all_gather | solution.py:85
  32.0 0.6 copy.30
  32.6 0.1 multiply_reduce_fusion.7
  32.8 0.8 copy-done
  33.8 6.6 %reduce-scatter.9.cloned.1.call-done = f32[256,256]{1,0:T(8,128)} async-done(((f32[1024,256]{1,0:T(8,128)}), f32[256,256]{1,0:T(8,128)}) %reduce-scatter.9.cloned.1.call-update) | async-done | bytes 262160 | tf_op jit(solution)/shard_map/reduce_scatter | solution.py:30
  40.4 1.1 multiply_reduce_fusion.2
  41.5 27.1 %reduce-scatter.11.cloned.1.call-done = f32[256,256]{1,0:T(8,128)} async-done(((f32[256,1024]{1,0:T(8,128)}), f32[256,256]{1,0:T(8,128)}) %reduce-scatter.11.cloned.1.call-update) | async-done | bytes 262160 | tf_op jit(solution)/shard_map/reduce_scatter | solution.py:31
  68.6 1.0 multiply_reduce_fusion
  69.6 27.1 %reduce-scatter.5.cloned.1.call-done = f32[256,256]{1,0:T(8,128)} async-done(((f32[1024,256]{1,0:T(8,128)}), f32[256,256]{1,0:T(8,128)}) %reduce-scatter.5.cloned.1.call-update) | async-done | bytes 262160 | tf_op jit(solution)/shard_map/reduce_scatter | solution.py:28
  96.7 1.1 multiply_reduce_fusion.6
  97.7 26.9 %reduce-scatter.7.cloned.1.call-done = f32[256,256]{1,0:T(8,128)} async-done(((f32[1024,256]{1,0:T(8,128)}), f32[256,256]{1,0:T(8,128)}) %reduce-scatter.7.cloned.1.call-update) | async-done | bytes 262160 | tf_op jit(solution)/shard_map/reduce_scatter | solution.py:29
  124.7 1.1 multiply_reduce_fusion.4
  125.8 10.0 %all-reduce = (f32[256,1]{0,1:T(1,128)S(1)}, f32[256,1]{0,1:T(1,128)S(1)}, f32[256,1]{0,1:T(1,128)S(1)}, f32[256,1]{0,1:T(1,128)S(1)}, f32[256,1]{0,1:T(1,128)S(...) all-reduce(f32[256,1]{0,1:T(1,128)S(1)} %bitcast.34, ...), channel_id=1, replica_groups=mesh['job'=2,'replica'=4,'model'=4] {'model'}, use_global_device_ids=true, to_apply=%region_4.0 | all-reduce | flops 2048 | bytes 16384 | tf_op jit(solution)/shard_map/psum | solution.py:53
  135.8 0.9 fusion.3
  136.7 14.8 %all_gather.16 = bf16[1024,256]{1,0:T(8,128)(2,1)S(1)} all-gather(bf16[256,256]{1,0:T(8,128)(2,1)S(1)} %get-tuple-element.32), channel_id=1, replica_groups=mesh['job'=2,'replica'=4,'model'=4] {'replica'}, dimensions={0}, use_global_device_ids=true | all-gather | bytes 655360 | tf_op jit(solution)/shard_map/all_gather | solution.py:82
  151.5 0.9 fusion.2
  152.4 15.3 %all_gather.17 = bf16[1024,256]{1,0:T(8,128)(2,1)S(1)} all-gather(bf16[256,256]{1,0:T(8,128)(2,1)S(1)} %get-tuple-element.29), channel_id=1, replica_groups=mesh['job'=2,'replica'=4,'model'=4] {'replica'}, dimensions={0}, use_global_device_ids=true | all-gather | bytes 655360 | tf_op jit(solution)/shard_map/all_gather | solution.py:83
  167.8 0.8 fusion.1
  168.6 16.1 %all_gather.18 = bf16[256,1024]{1,0:T(8,128)(2,1)S(1)} all-gather(bf16[256,256]{1,0:T(8,128)(2,1)S(1)} %get-tuple-element.26), channel_id=1, replica_groups=mesh['job'=2,'replica'=4,'model'=4] {'replica'}, dimensions={1}, use_global_device_ids=true | all-gather | bytes 655360 | tf_op jit(solution)/shard_map/all_gather | solution.py:84
  184.7 0.9 fusion.4
  185.7 14.8 %all_gather.15 = bf16[1024,256]{1,0:T(8,128)(2,1)S(1)} all-gather(bf16[256,256]{1,0:T(8,128)(2,1)S(1)} %get-tuple-element.35), channel_id=1, replica_groups=mesh['job'=2,'replica'=4,'model'=4] {'replica'}, dimensions={0}, use_global_device_ids=true | all-gather | bytes 655360 | tf_op jit(solution)/shard_map/all_gather | solution.py:81
  200.4 0.8 copy.35
  201.2 0.8 copy.36
  202.0 0.8 copy.37
  202.8 0.8 copy.38
  (40 shorter events, 0.6 us)
Async XLA Ops:
  7.2 33.2 %reduce-scatter.9.cloned.1.call-start = ((), (), s32[]{:S(2)}) async-start(), calls=%async_computation.6 | async-start | bytes 1310720 | tf_op jit(solution)/shard_map/reduce_scatter | solution.py:30
  7.9 60.6 %reduce-scatter.11.cloned.1.call-start = ((), (), s32[]{:S(2)}) async-start(), calls=%async_computation.7 | async-start | bytes 1310720 | tf_op jit(solution)/shard_map/reduce_scatter | solution.py:31
  8.7 88.0 %reduce-scatter.5.cloned.1.call-start = ((), (), s32[]{:S(2)}) async-start(), calls=%async_computation.4 | async-start | bytes 1310720 | tf_op jit(solution)/shard_map/reduce_scatter | solution.py:28
  9.4 115.2 %reduce-scatter.7.cloned.1.call-start = ((), (), s32[]{:S(2)}) async-start(), calls=%async_computation.5 | async-start | bytes 1310720 | tf_op jit(solution)/shard_map/reduce_scatter | solution.py:29
  9.4 0.7 copy-start.12
  9.5 14.1 %copy-start.13 = (f32[256]{0:T(256)S(1)}, f32[256]{0:T(256)}, u32[]{:S(2)}) copy-start(f32[256]{0:T(256)} %param.24) | copy-start | bytes 3076
  9.5 14.1 %copy-start.14 = (f32[256]{0:T(256)S(1)}, f32[256]{0:T(256)}, u32[]{:S(2)}) copy-start(f32[256]{0:T(256)} %param.29) | copy-start | bytes 3076
  9.5 23.1 %copy-start.3 = (f32[256,256]{1,0:T(8,128)S(1)}, f32[256,256]{1,0:T(8,128)}, u32[]{:S(2)}) copy-start(f32[256,256]{1,0:T(8,128)} %param.20) | copy-start | bytes 786436
  10.0 22.7 %copy-start.2 = (f32[256,256]{1,0:T(8,128)S(1)}, f32[256,256]{1,0:T(8,128)}, u32[]{:S(2)}) copy-start(f32[256,256]{1,0:T(8,128)} %param.23) | copy-start | bytes 786436
  32.6 1.0 copy-start
  32.7 1.0 copy-start.1
  69.6 66.2 %copy-start.8 = (f32[256,256]{1,0:T(8,128)S(1)}, f32[256,256]{1,0:T(8,128)}, u32[]{:S(2)}) copy-start(f32[256,256]{1,0:T(8,128)} %param.26) | copy-start | bytes 786436
  124.7 11.2 %copy-start.7 = (f32[256,256]{1,0:T(8,128)S(1)}, f32[256,256]{1,0:T(8,128)}, u32[]{:S(2)}) copy-start(f32[256,256]{1,0:T(8,128)} %reduce-scatter.7.cloned.1.call-done) | copy-start | bytes 786436
  136.7 14.8 %copy-start.6 = (f32[256,256]{1,0:T(8,128)S(1)}, f32[256,256]{1,0:T(8,128)}, u32[]{:S(2)}) copy-start(f32[256,256]{1,0:T(8,128)} %reduce-scatter.9.cloned.1.call-done) | copy-start | bytes 786436
  136.7 14.8 %copy-start.9 = (f32[256,256]{1,0:T(8,128)S(1)}, f32[256,256]{1,0:T(8,128)}, u32[]{:S(2)}) copy-start(f32[256,256]{1,0:T(8,128)} %param.27) | copy-start | bytes 786436
  152.4 15.3 %copy-start.5 = (f32[256,256]{1,0:T(8,128)S(1)}, f32[256,256]{1,0:T(8,128)}, u32[]{:S(2)}) copy-start(f32[256,256]{1,0:T(8,128)} %reduce-scatter.11.cloned.1.call-done) | copy-start | bytes 786436
  152.4 15.4 %copy-start.10 = (f32[256,256]{1,0:T(8,128)S(1)}, f32[256,256]{1,0:T(8,128)}, u32[]{:S(2)}) copy-start(f32[256,256]{1,0:T(8,128)} %param.28) | copy-start | bytes 786436
  168.6 16.1 %copy-start.4 = (f32[256,256]{1,0:T(8,128)S(1)}, f32[256,256]{1,0:T(8,128)}, u32[]{:S(2)}) copy-start(f32[256,256]{1,0:T(8,128)} %reduce-scatter.5.cloned.1.call-done) | copy-start | bytes 786436
  168.6 16.1 %copy-start.11 = (f32[256,256]{1,0:T(8,128)S(1)}, f32[256,256]{1,0:T(8,128)}, u32[]{:S(2)}) copy-start(f32[256,256]{1,0:T(8,128)} %param.25) | copy-start | bytes 786436
Sparse Core Ops, SparseCore 0:
  10.3 30.1 reduce-scatter.8
  42.7 25.7 reduce-scatter.10
  70.9 25.7 reduce-scatter.4
  98.8 25.7 reduce-scatter.6
where the time goes:
time: 210 us
  blocking collectives  92.1 us (44%)
  waiting for transfers between devices  90.2 us (43%)
  between operations  14 us (7%)
  other arithmetic  8.91 us (4%)
  local copies, waits for them, and re-layouts  4.75 us (2%)
    reduce_scatter x1, waiting for transfers between devices, local(): lax.psum_scatter(grad_query[0], 'replica', scatter_dimension=0, tiled=True)  27.1 us
    reduce_scatter x1, waiting for transfers between devices, local(): lax.psum_scatter(grad_mixed[0], 'replica', scatter_dimension=1, tiled=True)  27.1 us
    reduce_scatter x1, waiting for transfers between devices, local(): lax.psum_scatter(grad_key[0], 'replica', scatter_dimension=0, tiled=True)  26.9 us
    all_gather x1, blocking collectives, local(): lax.all_gather(new_mixed.astype(jnp.bfloat16), 'replica', axis=1, tiled=T...  16.1 us
    all_gather x1, blocking collectives, local(): lax.all_gather(new_value.astype(jnp.bfloat16), 'replica', axis=0, tiled=T...  15.3 us
    all_gather x1, blocking collectives, local(): lax.all_gather(new_key.astype(jnp.bfloat16), 'replica', axis=0, tiled=True)  14.8 us
    all_gather x1, blocking collectives, local(): lax.all_gather(new_query.astype(jnp.bfloat16), 'replica', axis=0, tiled=T...  14.8 us
    psum x1, blocking collectives, local(): whole_norm = lax.psum(grad_norm[0], 'replica')  13.5 us
  transfers between devices with their start and end apart: 4, of which 4 were waited for; matrix products, arithmetic and copies ran while one was open for 2% of the time, Pallas kernels for 0%

commit v1 on v0

--- a/solution.py
+++ b/solution.py
@@ -1,3 +1,4 @@
+import functools
 import jax
 import jax.numpy as jnp
 from jax import lax
@@ -5,6 +6,23 @@
 
 learn_rate = 0.5
 hold_rate = 0.9
+
+
+def start_paths(inp, chip_axis):
+    n = lax.axis_size(chip_axis)
+    vals = [(dev_i, (dev_i + 1) % n) for dev_i in range(n)]
+    log = [(dev_i, (dev_i - 1) % n) for dev_i in range(n)]
+    reached, then = ([inp], [inp])
+    for _ in range(n // 2):
+        reached.append(lax.ppermute(reached[-1], chip_axis, vals))
+    for _ in tuple(range((n - 1) // 2)):
+        then.append(lax.ppermute(then[-1], chip_axis, log))
+    vec_out = jnp.concatenate([*reached[::-1], *then[1:]], axis=0)
+    newest = jnp.roll(vec_out, (lax.axis_index(chip_axis) - n // 2) * inp.shape[0], axis=0)
+    return newest
+
+
+series_order = functools.partial(start_paths, chip_axis="replica")
 
 
 def local(
@@ -78,7 +96,7 @@
     state_new_norm = hold_rate * moment_norm + mean_norm
     new_norm = weight_norm - learn_rate * state_new_norm
     copy_query, copy_key, copy_value, copy_mixed, copy_norm = (
-        lax.all_gather(new_query.astype(jnp.bfloat16), "replica", axis=0, tiled=True),
+        series_order(new_query.astype(jnp.bfloat16)),
         lax.all_gather(new_key.astype(jnp.bfloat16), "replica", axis=0, tiled=True),
         lax.all_gather(new_value.astype(jnp.bfloat16), "replica", axis=0, tiled=True),
         lax.all_gather(new_mixed.astype(jnp.bfloat16), "replica", axis=1, tiled=True),

time: 210 us -> 201 us (0.957)
  blocking collectives: 92.1 us -> 79.1 us
  starting transfers between devices: 0.15 us -> 3.98 us
    all_gather x1 -> x0, blocking collectives: 14.8 us -> none  [local(): lax.all_gather(new_query.astype(jnp.bfloat16), 'replica', axis=0, tiled=T...]
    ppermute x0 -> x3, starting transfers between devices: none -> 3.83 us  [the longest x1 3.82 us: start_paths(): then.append(lax.ppermute(then[-1], chip_axis, log))]
    unnamed x36 -> x42, local copies, waits for them, and re-layouts: 4.75 us -> 4.02 us
  transfers between devices with their start and end apart: 4 -> 7, of which waited for: 4 -> 4; matrix products, arithmetic and copies ran while one was open for 2% -> 4% of each run, Pallas kernels for 0% -> 0%
where the time goes in v1:
time: 201 us
  waiting for transfers between devices  90.2 us (45%)
  blocking collectives  79.1 us (39%)
  between operations  14.1 us (7%)
  other arithmetic  8.91 us (4%)
  local copies, waits for them, and re-layouts  4.86 us (2%)
  starting transfers between devices  3.98 us (2%)
    reduce_scatter x1, waiting for transfers between devices, local(): lax.psum_scatter(grad_query[0], 'replica', scatter_dimension=0, tiled=True)  27.1 us
    reduce_scatter x1, waiting for transfers between devices, local(): lax.psum_scatter(grad_mixed[0], 'replica', scatter_dimension=1, tiled=True)  27.1 us
    reduce_scatter x1, waiting for transfers between devices, local(): lax.psum_scatter(grad_key[0], 'replica', scatter_dimension=0, tiled=True)  26.8 us
    all_gather x1, blocking collectives, local(): lax.all_gather(new_mixed.astype(jnp.bfloat16), 'replica', axis=1, tiled=T...  16.6 us
    all_gather x1, blocking collectives, local(): lax.all_gather(new_value.astype(jnp.bfloat16), 'replica', axis=0, tiled=T...  16.1 us
    all_gather x1, blocking collectives, local(): lax.all_gather(new_key.astype(jnp.bfloat16), 'replica', axis=0, tiled=True)  15.2 us
    psum x1, blocking collectives, local(): whole_norm = lax.psum(grad_norm[0], 'replica')  13.5 us
    psum x1, blocking collectives, local(): lax.psum((jnp.sum(weight_query * weight_query, axis=1, keepdims=True), jn...  9.98 us
  transfers between devices with their start and end apart: 7, of which 4 were waited for; matrix products, arithmetic and copies ran while one was open for 4% of the time, Pallas kernels for 0%

profile of v1, /device:TPU:0, one launch (start us, length us, event | category | flops | bytes accessed | tf_op | source)
XLA Modules:
  0.0 201.1 jit_solution(10303013348562320321)
XLA Ops:
  7.2 0.7 reduce-scatter.9.cloned.1.call-update
  8.0 0.7 reduce-scatter.11.cloned.1.call-update
  8.7 0.7 reduce-scatter.5.cloned.1.call-update
  9.5 0.5 reduce-scatter.7.cloned.1.call-update
  10.0 0.1 copy-done.12
  10.1 13.5 %psum.71 = f32[1024]{0:T(1024)S(1)} all-reduce(f32[1024]{0:T(1024)S(1)} %bitcast.36), channel_id=1, replica_groups=mesh['job'=2,'replica'=4,'model'=4] {'replica'}, use_global_device_ids=true, to_apply=%region_20.0 | all-reduce | flops 1024 | bytes 8192 | tf_op jit(solution)/shard_map/psum | solution.py:51
  23.6 0.6 fusion
  24.3 7.7 %all-gather = bf16[4,1,256]{2,1,0:T(2,128)(2,1)S(1)} all-gather(bf16[1,1,256]{2,1,0:T(2,128)(2,1)S(1)} %reshape.38), channel_id=1, replica_groups=mesh['job'=2,'replica'=4,'model'=4] {'replica'}, dimensions={0}, use_global_device_ids=true | all-gather | bytes 2560 | tf_op jit(solution)/shard_map/all_gather | solution.py:103
  32.0 0.6 copy.30
  32.6 0.1 multiply_reduce_fusion.7
  32.8 0.8 copy-done.1
  33.8 6.6 %reduce-scatter.9.cloned.1.call-done = f32[256,256]{1,0:T(8,128)} async-done(((f32[1024,256]{1,0:T(8,128)}), f32[256,256]{1,0:T(8,128)}) %reduce-scatter.9.cloned.1.call-update) | async-done | bytes 262160 | tf_op jit(solution)/shard_map/reduce_scatter | solution.py:48
  40.4 1.1 multiply_reduce_fusion.2
  41.5 27.1 %reduce-scatter.11.cloned.1.call-done = f32[256,256]{1,0:T(8,128)} async-done(((f32[256,1024]{1,0:T(8,128)}), f32[256,256]{1,0:T(8,128)}) %reduce-scatter.11.cloned.1.call-update) | async-done | bytes 262160 | tf_op jit(solution)/shard_map/reduce_scatter | solution.py:49
  68.6 1.0 multiply_reduce_fusion
  69.6 27.1 %reduce-scatter.5.cloned.1.call-done = f32[256,256]{1,0:T(8,128)} async-done(((f32[1024,256]{1,0:T(8,128)}), f32[256,256]{1,0:T(8,128)}) %reduce-scatter.5.cloned.1.call-update) | async-done | bytes 262160 | tf_op jit(solution)/shard_map/reduce_scatter | solution.py:46
  96.7 1.1 multiply_reduce_fusion.6
  97.8 26.8 %reduce-scatter.7.cloned.1.call-done = f32[256,256]{1,0:T(8,128)} async-done(((f32[1024,256]{1,0:T(8,128)}), f32[256,256]{1,0:T(8,128)}) %reduce-scatter.7.cloned.1.call-update) | async-done | bytes 262160 | tf_op jit(solution)/shard_map/reduce_scatter | solution.py:47
  124.7 1.1 multiply_reduce_fusion.4
  125.7 10.0 %all-reduce = (f32[256,1]{0,1:T(1,128)S(1)}, f32[256,1]{0,1:T(1,128)S(1)}, f32[256,1]{0,1:T(1,128)S(1)}, f32[256,1]{0,1:T(1,128)S(1)}, f32[256,1]{0,1:T(1,128)S(...) all-reduce(f32[256,1]{0,1:T(1,128)S(1)} %bitcast.34, ...), channel_id=1, replica_groups=mesh['job'=2,'replica'=4,'model'=4] {'model'}, use_global_device_ids=true, to_apply=%region_4.0 | all-reduce | flops 2048 | bytes 16384 | tf_op jit(solution)/shard_map/psum | solution.py:71
  135.8 0.9 fusion.4
  136.7 3.8 %collective-permute-start.2 = (bf16[256,256]{1,0:T(8,128)(2,1)S(1)}, bf16[256,256]{1,0:T(8,128)(2,1)S(1)}, u32[]{:S(2)}, u32[]{:S(2)}) collective-permute-start(bf16[256,256]{1,0:T(8,128)(2,1)S(1)} %get-tuple-element.35), channel_id=1, source_target_pairs={{0,12},{4,0},{8,4},{12,8},{1,13},{5,1},{9,5},{13,9},{2,14},{6,2},{... | collective-permute-start | bytes 393224 | tf_op jit(solution)/shard_map/ppermute | solution.py:19
  140.5 0.9 fusion.3
  141.4 15.2 %all_gather.12 = bf16[1024,256]{1,0:T(8,128)(2,1)S(1)} all-gather(bf16[256,256]{1,0:T(8,128)(2,1)S(1)} %get-tuple-element.32), channel_id=1, replica_groups=mesh['job'=2,'replica'=4,'model'=4] {'replica'}, dimensions={0}, use_global_device_ids=true | all-gather | bytes 655360 | tf_op jit(solution)/shard_map/all_gather | solution.py:100
  156.7 0.9 fusion.2
  157.6 16.1 %all_gather.13 = bf16[1024,256]{1,0:T(8,128)(2,1)S(1)} all-gather(bf16[256,256]{1,0:T(8,128)(2,1)S(1)} %get-tuple-element.29), channel_id=1, replica_groups=mesh['job'=2,'replica'=4,'model'=4] {'replica'}, dimensions={0}, use_global_device_ids=true | all-gather | bytes 655360 | tf_op jit(solution)/shard_map/all_gather | solution.py:101
  173.7 0.8 fusion.1
  174.6 16.6 %all_gather.14 = bf16[256,1024]{1,0:T(8,128)(2,1)S(1)} all-gather(bf16[256,256]{1,0:T(8,128)(2,1)S(1)} %get-tuple-element.26), channel_id=1, replica_groups=mesh['job'=2,'replica'=4,'model'=4] {'replica'}, dimensions={1}, use_global_device_ids=true | all-gather | bytes 655360 | tf_op jit(solution)/shard_map/all_gather | solution.py:102
  191.3 0.8 constant_dynamic-slice_fusion
  192.2 0.8 copy.41
  193.0 0.8 copy.42
  193.7 0.8 copy.43
  (53 shorter events, 0.7 us)
Async XLA Ops:
  7.2 33.2 %reduce-scatter.9.cloned.1.call-start = ((), (), s32[]{:S(2)}) async-start(), calls=%async_computation.6 | async-start | bytes 1310720 | tf_op jit(solution)/shard_map/reduce_scatter | solution.py:48
  7.9 60.6 %reduce-scatter.11.cloned.1.call-start = ((), (), s32[]{:S(2)}) async-start(), calls=%async_computation.7 | async-start | bytes 1310720 | tf_op jit(solution)/shard_map/reduce_scatter | solution.py:49
  8.7 88.0 %reduce-scatter.5.cloned.1.call-start = ((), (), s32[]{:S(2)}) async-start(), calls=%async_computation.4 | async-start | bytes 1310720 | tf_op jit(solution)/shard_map/reduce_scatter | solution.py:46
  9.4 115.2 %reduce-scatter.7.cloned.1.call-start = ((), (), s32[]{:S(2)}) async-start(), calls=%async_computation.5 | async-start | bytes 1310720 | tf_op jit(solution)/shard_map/reduce_scatter | solution.py:47
  9.4 0.7 copy-start.12
  9.5 14.1 %copy-start.13 = (f32[256]{0:T(256)S(1)}, f32[256]{0:T(256)}, u32[]{:S(2)}) copy-start(f32[256]{0:T(256)} %param.24) | copy-start | bytes 3076
  9.5 14.1 %copy-start.14 = (f32[256]{0:T(256)S(1)}, f32[256]{0:T(256)}, u32[]{:S(2)}) copy-start(f32[256]{0:T(256)} %param.29) | copy-start | bytes 3076
  9.5 23.1 %copy-start = (f32[256,256]{1,0:T(8,128)S(1)}, f32[256,256]{1,0:T(8,128)}, u32[]{:S(2)}) copy-start(f32[256,256]{1,0:T(8,128)} %param.20) | copy-start | bytes 786436
  10.0 22.7 %copy-start.3 = (f32[256,256]{1,0:T(8,128)S(1)}, f32[256,256]{1,0:T(8,128)}, u32[]{:S(2)}) copy-start(f32[256,256]{1,0:T(8,128)} %param.23) | copy-start | bytes 786436
  32.6 1.0 copy-start.1
  32.7 1.0 copy-start.2
  69.6 66.2 %copy-start.8 = (f32[256,256]{1,0:T(8,128)S(1)}, f32[256,256]{1,0:T(8,128)}, u32[]{:S(2)}) copy-start(f32[256,256]{1,0:T(8,128)} %param.25) | copy-start | bytes 786436
  96.7 39.1 %copy-start.7 = (f32[256,256]{1,0:T(8,128)S(1)}, f32[256,256]{1,0:T(8,128)}, u32[]{:S(2)}) copy-start(f32[256,256]{1,0:T(8,128)} %reduce-scatter.5.cloned.1.call-done) | copy-start | bytes 786436
  135.7 4.8 %copy-start.6 = (f32[256,256]{1,0:T(8,128)S(1)}, f32[256,256]{1,0:T(8,128)}, u32[]{:S(2)}) copy-start(f32[256,256]{1,0:T(8,128)} %reduce-scatter.7.cloned.1.call-done) | copy-start | bytes 786436
  135.8 4.8 %copy-start.9 = (f32[256,256]{1,0:T(8,128)S(1)}, f32[256,256]{1,0:T(8,128)}, u32[]{:S(2)}) copy-start(f32[256,256]{1,0:T(8,128)} %param.26) | copy-start | bytes 786436
  136.7 37.9 %collective-permute-start = (bf16[256,256]{1,0:T(8,128)(2,1)S(1)}, bf16[256,256]{1,0:T(8,128)(2,1)S(1)}, u32[]{:S(2)}, u32[]{:S(2)}) collective-permute-start(bf16[256,256]{1,0:T(8,128)(2,1)S(1)} %get-tuple-element.35), channel_id=1, source_target_pairs={{0,4},{4,8},{8,12},{12,0},{1,5},{5,9},{9,13},{13,1},{2,6},{6,10},{... | collective-permute-start | bytes 393224 | tf_op jit(solution)/shard_map/ppermute | solution.py:17
  136.7 54.6 %collective-permute-start.2 = (bf16[256,256]{1,0:T(8,128)(2,1)S(1)}, bf16[256,256]{1,0:T(8,128)(2,1)S(1)}, u32[]{:S(2)}, u32[]{:S(2)}) collective-permute-start(bf16[256,256]{1,0:T(8,128)(2,1)S(1)} %get-tuple-element.35), channel_id=1, source_target_pairs={{0,12},{4,0},{8,4},{12,8},{1,13},{5,1},{9,5},{13,9},{2,14},{6,2},{... | collective-permute-start | bytes 393224 | tf_op jit(solution)/shard_map/ppermute | solution.py:19
  141.4 15.2 %copy-start.5 = (f32[256,256]{1,0:T(8,128)S(1)}, f32[256,256]{1,0:T(8,128)}, u32[]{:S(2)}) copy-start(f32[256,256]{1,0:T(8,128)} %reduce-scatter.9.cloned.1.call-done) | copy-start | bytes 786436
  141.4 15.3 %copy-start.10 = (f32[256,256]{1,0:T(8,128)S(1)}, f32[256,256]{1,0:T(8,128)}, u32[]{:S(2)}) copy-start(f32[256,256]{1,0:T(8,128)} %param.27) | copy-start | bytes 786436
  157.6 16.1 %copy-start.4 = (f32[256,256]{1,0:T(8,128)S(1)}, f32[256,256]{1,0:T(8,128)}, u32[]{:S(2)}) copy-start(f32[256,256]{1,0:T(8,128)} %reduce-scatter.11.cloned.1.call-done) | copy-start | bytes 786436
  157.6 16.1 %copy-start.11 = (f32[256,256]{1,0:T(8,128)S(1)}, f32[256,256]{1,0:T(8,128)}, u32[]{:S(2)}) copy-start(f32[256,256]{1,0:T(8,128)} %param.28) | copy-start | bytes 786436
  174.6 16.6 %collective-permute-start.1 = (bf16[256,256]{1,0:T(8,128)(2,1)S(1)}, bf16[256,256]{1,0:T(8,128)(2,1)S(1)}, u32[]{:S(2)}, u32[]{:S(2)}) collective-permute-start(bf16[256,256]{1,0:T(8,128)(2,1)S(1)} %collective-permute-done), channel_id=1, source_target_pairs={{0,4},{4,8},{8,12},{12,0},{1,5},{5,9},{9,13},{13,1},{2,6},{6,10},{... | collective-permute-start | bytes 393224 | tf_op jit(solution)/shard_map/ppermute | solution.py:17
Sparse Core Ops, SparseCore 0:
  10.3 30.1 reduce-scatter.8
  42.7 25.7 reduce-scatter.10
  70.9 25.7 reduce-scatter.4
  98.8 25.7 reduce-scatter.6
